TPU v7x, 128 devices: a whole 4x4x4 slice. The times are simulated.
128 devices in a mesh: chan: 4 (over x_lo, core), slab: 32 (over y, z, x_hi).
Axes of the slice: x: 4 (x_hi: 2, x_lo: 2; x = x_hi * 2 + x_lo), y: 4, z: 4, core: 2. Of those that a mesh axis runs over, the one named last changes fastest.
Arguments:
- beam_images: float32 [64, 2048, 4096], P('chan', 'slab'), may hold values from -24 to 24
- chan_weights: int32 [64], P('chan'), may hold values from 1 to 8
- freq_offsets: float32 [64], P('chan'), may hold values from -1 to 1
- half_widths: int32 [5], replicated, may hold values from 16 to 32, as said below
Outputs:
- smoothed: float32 [5, 2048, 4096], P(None, 'slab', 'chan')
Inputs may be any that keep to these rules, and one draw needn't show every extreme that they name: `half_widths`: each half-width is at least 16 and at most 32; at least one equals 32.
All inputs are finite; a program needn't handle non-finite values.
Results may differ from a plain program's by a relative error of at most 0.00008.
Values sent between devices are 32-bit elements; how exact they have to be, the bound alone decides.
A program may use at most 128 MiB of HBM per device.

v0:
```python
import jax
import jax.numpy as jnp
from jax import lax
from jax.sharding import PartitionSpec as P

MOMENTS = 5
HW_MAX = 32


def sent_to_all(array, axis):
    copies = jnp.broadcast_to(array, (lax.axis_size(axis), *array.shape))
    return lax.all_to_all(copies, axis, split_axis=0, concat_axis=0, tiled=True)


def of_everyone(array, axis):
    everything = sent_to_all(array, axis)
    return jnp.sum(everything, axis=0)


def padded(cells, sides, width):
    for axis, dim in sides:
        count = lax.axis_size(axis)
        ends = count - 1
        head = lax.slice_in_dim(cells, 0, width, axis=dim)
        tail = lax.slice_in_dim(cells, cells.shape[dim] - width, cells.shape[dim], axis=dim)
        cells = jnp.concatenate(
            [
                lax.ppermute(tail, axis, [(i, (i + 1) % count) for i in range(ends)]),
                cells,
                lax.ppermute(head, axis, [((i + 1) % count, i) for i in range(ends)]),
            ],
            axis=dim,
        )
    return cells


def row_pass(extended, half_widths):
    total_rows = extended.shape[1]
    out_rows = total_rows - 2 * HW_MAX
    out_index = lax.broadcasted_iota(jnp.int32, (out_rows, total_rows), 0)
    in_index = lax.broadcasted_iota(jnp.int32, (out_rows, total_rows), 1)
    distance = jnp.abs(in_index - HW_MAX - out_index)
    row_band = (distance[None] <= half_widths[:, None, None]).astype(jnp.float32)
    return jnp.einsum(
        "kim,kmj->kij",
        row_band,
        extended,
        precision=lax.Precision.HIGHEST,
        preferred_element_type=jnp.float32,
    )


def column_pass(extended, half_widths):
    total_cols = extended.shape[2]
    out_cols = total_cols - 2 * HW_MAX
    in_index = lax.broadcasted_iota(jnp.int32, (total_cols, out_cols), 0)
    out_index = lax.broadcasted_iota(jnp.int32, (total_cols, out_cols), 1)
    distance = jnp.abs(in_index - HW_MAX - out_index)
    col_band = (distance[None] <= half_widths[:, None, None]).astype(jnp.float32)
    return jnp.einsum(
        "kim,kmj->kij",
        extended,
        col_band,
        precision=lax.Precision.HIGHEST,
        preferred_element_type=jnp.float32,
    )


def body(beam_images, chan_weights, freq_offsets, half_widths):
    local_chans = beam_images.shape[0]
    slab_rows = beam_images.shape[1]
    all_cols = beam_images.shape[2]
    weight_floats = chan_weights.astype(jnp.float32)
    weight_total = of_everyone(jnp.sum(weight_floats), "chan")
    powers = jnp.stack([freq_offsets**power for power in range(MOMENTS)])
    coefficients = powers * weight_floats[None, :] / weight_total
    flat = beam_images.reshape(local_chans, slab_rows * all_cols)
    partials = jnp.dot(
        coefficients, flat, precision=lax.Precision.HIGHEST, preferred_element_type=jnp.float32
    )
    partials = partials.reshape(MOMENTS, slab_rows, all_cols)
    shares = lax.psum_scatter(partials, "chan", scatter_dimension=2, tiled=True)
    extended = padded(shares, (("chan", 2), ("slab", 1)), HW_MAX)
    summed = column_pass(row_pass(extended, half_widths), half_widths)
    divisor = (2 * half_widths + 1).astype(jnp.float32)
    return summed / divisor[:, None, None]


def solution(mesh):
    placed = (P("chan", "slab", None), P("chan"), P("chan"), P())
    return jax.shard_map(
        body, mesh=mesh, in_specs=placed, out_specs=P(None, "slab", "chan"), check_vma=False
    )
```

profile of v0, /device:TPU:1, one launch (start us, length us, event | category | flops | bytes accessed | tf_op | source)
XLA Modules:
  0.0 192.5 jit_solution(1530563390376721928)
XLA Ops:
  6.5 1.3 convert_reduce_fusion
  7.8 1.2 broadcast_in_dim.2
  9.0 4.6 %all-to-all-start = ((f32[4,1,1]{2,1,0:T(1,128)}), f32[4,1,1]{2,1,0:T(1,128)S(1)}, u32[]{:S(2)}, u32[]{:S(2)}) async-start(f32[4,1,1]{2,1,0:T(1,128)} %broadcast_in_dim.2), calls=%async_computation | async-start | bytes 4096 | tf_op jit(solution)/shard_map/all_to_all | solution.py:12
  13.6 0.7 convert_element_type.8
  14.2 0.7 multiply_bitcast_fusion
  14.9 0.7 stack.19
  15.6 1.0 all-to-all-done
  16.6 0.6 reduce_sum.19
  17.2 25.8 %fusion.2 = f32[5,64,4096]{2,0,1:T(8,128)} fusion(f32[5,16]{1,0:T(8,128)S(1)} %stack.19, f32[]{:T(128)} %reduce_sum.19, f32[16]{0:T(128)S(1)} %convert_element_type.8, f32[2,8,64,4096]{3,2,1,0:T(8,128)} %bitcast.22), kind=kOutput, calls=%fused_computation.2 | convolution fusion | flops 251658400 | bytes 22020484 | tf_op jit(solution)/shard_map/dot_general | solution.py:78
  43.0 81.9 %reduce-scatter.2.cloned.1.call-done = f32[5,64,1024]{2,0,1:T(8,128)} async-done(((f32[5,64,4096]{2,0,1:T(8,128)}), f32[5,64,1024]{2,0,1:T(8,128)}) %reduce-scatter.2.cloned.1.call-update) | async-done | bytes 1310736 | tf_op jit(solution)/shard_map/reduce_scatter | solution.py:82
  124.9 1.2 fusion.21
  126.1 2.1 %collective-permute-start = (f32[5,64,32]{2,0,1:T(8,128)S(1)}, f32[5,64,32]{2,0,1:T(8,128)S(1)}, u32[]{:S(2)}, u32[]{:S(2)}) collective-permute-start(f32[5,64,32]{2,0,1:T(8,128)S(1)} %get-tuple-element.8), channel_id=1, source_target_pairs={{0,32},{32,64},{64,96},{1,33},{33,65},{65,97},{2,34},{34,66},{66,9... | collective-permute-start | bytes 122888 | tf_op jit(solution)/shard_map/ppermute | solution.py:28
  128.2 2.2 %collective-permute-start.1 = (f32[5,64,32]{2,0,1:T(8,128)S(1)}, f32[5,64,32]{2,0,1:T(8,128)S(1)}, u32[]{:S(2)}, u32[]{:S(2)}) collective-permute-start(f32[5,64,32]{2,0,1:T(8,128)S(1)} %get-tuple-element.7), channel_id=1, source_target_pairs={{32,0},{64,32},{96,64},{33,1},{65,33},{97,65},{34,2},{66,34},{98,6... | collective-permute-start | bytes 122888 | tf_op jit(solution)/shard_map/ppermute | solution.py:30
  130.5 1.0 collective-permute-done
  131.5 4.4 %collective-permute-done.1 = f32[5,64,32]{2,0,1:T(8,128)S(1)} collective-permute-done((f32[5,64,32]{2,0,1:T(8,128)S(1)}, f32[5,64,32]{2,0,1:T(8,128)S(1)}, u32[]{:S(2)}, u32[]{:S(2)}) %collective-permute-start.1) | collective-permute-done | bytes 40992 | tf_op jit(solution)/shard_map/ppermute | solution.py:30
  135.9 3.1 %concatenate.6 = f32[5,64,1088]{2,0,1:T(8,128)S(1)} concatenate(f32[5,64,32]{2,0,1:T(8,128)S(1)} %collective-permute-done, f32[5,64,1024]{2,0,1:T(8,128)} %reduce-scatter.2.cloned.1.call-done, f32[5,64,32]{2,0,1:T(8,128)S(1)} %collective-permute-done.1), dimensions={2} | concatenate | bytes 2785280 | tf_op jit(solution)/shard_map/concatenate | solution.py:26
  139.3 5.0 %collective-permute-start.2 = (f32[5,32,1088]{2,1,0:T(8,128)S(1)}, f32[5,32,1088]{2,1,0:T(8,128)S(1)}, u32[]{:S(2)}, u32[]{:S(2)}) collective-permute-start(f32[5,32,1088]{2,1,0:T(8,128)S(1)} %copy.20), channel_id=1, source_target_pairs={{0,1},{1,2},{2,3},{3,4},{4,5},{5,6},{6,7},{7,8},{8,9},{9,10},{10,1... | collective-permute-start | bytes 2088968 | tf_op jit(solution)/shard_map/ppermute | solution.py:28
  144.4 1.5 collective-permute-start.3
  145.9 0.6 subtract_abs_fusion
  146.6 10.2 %collective-permute-done.2 = f32[5,32,1088]{2,1,0:T(8,128)S(1)} collective-permute-done((f32[5,32,1088]{2,1,0:T(8,128)S(1)}, f32[5,32,1088]{2,1,0:T(8,128)S(1)}, u32[]{:S(2)}, u32[]{:S(2)}) %collective-permute-start.2) | collective-permute-done | bytes 696352 | tf_op jit(solution)/shard_map/ppermute | solution.py:28
  157.2 17.0 %collective-permute-done.3 = f32[5,32,1088]{2,1,0:T(8,128)S(1)} collective-permute-done((f32[5,32,1088]{2,1,0:T(8,128)S(1)}, f32[5,32,1088]{2,1,0:T(8,128)S(1)}, u32[]{:S(2)}, u32[]{:S(2)}) %collective-permute-start.3) | collective-permute-done | bytes 696352 | tf_op jit(solution)/shard_map/ppermute | solution.py:30
  174.7 0.5 pad_maximum_fusion
  175.2 1.5 fusion.7
  176.7 9.0 %fusion.9 = f32[5,64,1024]{2,1,0:T(8,128)} fusion(f32[5,64,1088]{2,1,0:T(8,128)S(1)} %fusion.7, s32[1088,1024]{1,0:T(8,128)S(1)} %subtract_abs_fusion, s32[5]{0:T(128)S(1)} %copy-done, f32[5]{0:T(128)S(1)} %add_convert_fusion), kind=kOutput, calls=%fused_computation.11 | convolution fusion | flops 4284088320 | bytes 7159848 | tf_op jit(solution)/shard_map/kim,kmj->kij/dot_general | solution.py:60
  (14 shorter events, 1.4 us)
Async XLA Ops:
  9.0 7.6 %all-to-all-start = ((f32[4,1,1]{2,1,0:T(1,128)}), f32[4,1,1]{2,1,0:T(1,128)S(1)}, u32[]{:S(2)}, u32[]{:S(2)}) async-start(f32[4,1,1]{2,1,0:T(1,128)} %broadcast_in_dim.2), calls=%async_computation | async-start | bytes 4096 | tf_op jit(solution)/shard_map/all_to_all | solution.py:12
  13.6 111.3 %reduce-scatter.2.cloned.1.call-start = ((), (), s32[]{:S(2)}) async-start(), calls=%async_computation.2 | async-start | bytes 10485760 | tf_op jit(solution)/shard_map/reduce_scatter | solution.py:82
  43.0 87.5 %copy-start = (s32[5]{0:T(128)S(1)}, s32[5]{0:T(128)}, u32[]{:S(2)}) copy-start(s32[5]{0:T(128)} %param.7) | copy-start | bytes 64
  126.1 5.4 %collective-permute-start = (f32[5,64,32]{2,0,1:T(8,128)S(1)}, f32[5,64,32]{2,0,1:T(8,128)S(1)}, u32[]{:S(2)}, u32[]{:S(2)}) collective-permute-start(f32[5,64,32]{2,0,1:T(8,128)S(1)} %get-tuple-element.8), channel_id=1, source_target_pairs={{0,32},{32,64},{64,96},{1,33},{33,65},{65,97},{2,34},{34,66},{66,9... | collective-permute-start | bytes 122888 | tf_op jit(solution)/shard_map/ppermute | solution.py:28
  128.2 7.7 %collective-permute-start.1 = (f32[5,64,32]{2,0,1:T(8,128)S(1)}, f32[5,64,32]{2,0,1:T(8,128)S(1)}, u32[]{:S(2)}, u32[]{:S(2)}) collective-permute-start(f32[5,64,32]{2,0,1:T(8,128)S(1)} %get-tuple-element.7), channel_id=1, source_target_pairs={{32,0},{64,32},{96,64},{33,1},{65,33},{97,65},{34,2},{66,34},{98,6... | collective-permute-start | bytes 122888 | tf_op jit(solution)/shard_map/ppermute | solution.py:30
  139.3 17.4 %collective-permute-start.2 = (f32[5,32,1088]{2,1,0:T(8,128)S(1)}, f32[5,32,1088]{2,1,0:T(8,128)S(1)}, u32[]{:S(2)}, u32[]{:S(2)}) collective-permute-start(f32[5,32,1088]{2,1,0:T(8,128)S(1)} %copy.20), channel_id=1, source_target_pairs={{0,1},{1,2},{2,3},{3,4},{4,5},{5,6},{6,7},{7,8},{8,9},{9,10},{10,1... | collective-permute-start | bytes 2088968 | tf_op jit(solution)/shard_map/ppermute | solution.py:28
  144.4 29.8 %collective-permute-start.3 = (f32[5,32,1088]{2,1,0:T(8,128)S(1)}, f32[5,32,1088]{2,1,0:T(8,128)S(1)}, u32[]{:S(2)}, u32[]{:S(2)}) collective-permute-start(f32[5,32,1088]{2,1,0:T(8,128)S(1)} %copy.21), channel_id=1, source_target_pairs={{1,0},{2,1},{3,2},{4,3},{5,4},{6,5},{7,6},{8,7},{9,8},{10,9},{11,1... | collective-permute-start | bytes 2088968 | tf_op jit(solution)/shard_map/ppermute | solution.py:30
Sparse Core Ops, SparseCore 0:
  43.1 81.7 reduce-scatter.1
where the time goes:
time: 193 us
  waiting for transfers between devices  116 us (60%)
  matrix products  36.3 us (19%)
  starting transfers between devices  15.4 us (8%)
  between operations  13.5 us (7%)
  local copies, waits for them, and re-layouts  7.46 us (4%)
  other arithmetic  4.33 us (2%)
    reduce_scatter x1, waiting for transfers between devices, body(): shares = lax.psum_scatter(partials, 'chan', scatter_dimension=2, tiled=True)  81.9 us
    dot_general x1, matrix products, body(): jnp.dot(coefficients, flat, precision=lax.Precision.HIGHEST, preferred_el...  25.8 us
    ppermute x2, waiting for transfers between devices, padded(): lax.ppermute(head, axis, [((i + 1) % count, i) for i in range(ends)])  21.4 us
    ppermute x2, waiting for transfers between devices, padded(): lax.ppermute(tail, axis, [(i, (i + 1) % count) for i in range(ends)])  11.2 us
    dot_general x1, matrix products, column_pass(): jnp.einsum('kim,kmj->kij', extended, col_band, precision=lax.Precision.HI...  9 us
    ppermute x2, starting transfers between devices, padded(): lax.ppermute(tail, axis, [(i, (i + 1) % count) for i in range(ends)])  7.08 us
    all_to_all x1, starting transfers between devices, sent_to_all(): return lax.all_to_all(copies, axis, split_axis=0, concat_axis=0, tiled=True)  4.57 us
  transfers between devices with their start and end apart: 6, of which 6 were waited for; matrix products, arithmetic and copies ran while one was open for 2% of the time, Pallas kernels for 0%

commit v1 on v0

v1 whole, which is shorter than its diff:
```python
import functools

import jax
import jax.numpy as jnp
from jax import lax
from jax.experimental import pallas as pl
from jax.experimental.pallas import tpu as pltpu
from jax.sharding import PartitionSpec as P

MESH = pl.DeviceIdType.MESH
MOMENTS = 5
HW = 32
LANES = 128
F32 = jnp.float32
BF16 = jnp.bfloat16


def halves(value):
    high = value.astype(BF16)
    low = (value - high.astype(F32)).astype(BF16)
    return high, low


def kernel(
    slabs, tiles, chans,
    beam, weights, offsets, reach, out,
    pix, part, got, from_same_far, from_same_own, from_direct, to_other, from_other,
    to_direct, from_rows, rows, done, row_band, col_band, coef, w_mine, w_got,
    pix_sem, core_send, core_recv, far_send, far_recv, own_send, own_recv,
    dir_send, dir_recv, oth_send, oth_recv, row_send, row_recv,
    edge_send, edge_recv, w_send, w_recv, out_sem,
):
    chan = lax.axis_index("chan")
    slab = lax.axis_index("slab")
    odd = slab % 2
    partner = (chan + 2) % 4
    other_core = chan + 1 - 2 * (chan % 2)
    far_core = 3 - chan
    same_slab = slab + 1 - 2 * odd
    other_slab = (slab + slabs - 1 + 2 * odd) % slabs
    half_same = 1 - odd
    half_other = odd
    to_core = (other_core, slab)
    to_partner = (partner, slab)
    to_far_core = (far_core, slab)
    to_wrap = (partner, same_slab)
    to_wrap_other = (partner, other_slab)

    def tile_of(order):
        return (tiles - order) % tiles

    def pixels(t, slot):
        quarter = (other_core, far_core, chan, partner)[slot]
        start = pl.multiple_of((quarter * tiles + t) * LANES, LANES)
        return pltpu.make_async_copy(beam.at[:, :, pl.ds(start, LANES)], pix.at[t, slot], pix_sem.at[t, slot])

    def remote(src, dst, send, recv, where):
        return pltpu.make_async_remote_copy(
            src_ref=src, dst_ref=dst, send_sem=send, recv_sem=recv, device_id=where, device_id_type=MESH
        )

    def core_copy(t):
        return remote(part.at[t, pl.ds(0, 2)], got.at[t], core_send.at[t], core_recv.at[t], to_core)

    def far_copy(t):
        return remote(part.at[t, 2, half_same], from_same_far.at[t], far_send.at[t], far_recv.at[t], to_wrap)

    def own_copy(t):
        return remote(part.at[t, 3, half_same], from_same_own.at[t], own_send.at[t], own_recv.at[t], to_wrap)

    def direct_copy(t):
        return remote(part.at[t, 2, half_other], from_direct.at[t], dir_send.at[t], dir_recv.at[t], to_partner)

    def other_copy(t):
        return remote(to_other.at[t], from_other.at[t], oth_send.at[t], oth_recv.at[t], to_wrap_other)

    def row_copy(t):
        return remote(to_direct.at[t], from_rows.at[t], row_send.at[t], row_recv.at[t], to_partner)

    def left_edge():
        return remote(rows.at[1], rows.at[tiles + 1], edge_send.at[0], edge_recv.at[1], ((chan + 3) % 4, slab))

    def right_edge():
        return remote(rows.at[tiles], rows.at[0], edge_send.at[1], edge_recv.at[0], ((chan + 1) % 4, slab))

    def weight_copy(i):
        return remote(w_mine, w_got.at[i], w_send.at[i], w_recv.at[i], (to_core, to_partner, to_far_core)[i])

    def result(t):
        start = pl.multiple_of(t * LANES, LANES)
        return pltpu.make_async_copy(done.at[t], out.at[:, :, pl.ds(start, LANES)], out_sem.at[t])

    def each(first, last, body):
        def step(order, carry):
            body(tile_of(order))
            return carry

        lax.fori_loop(first, last, step, 0)

    def fetch(t):
        for slot in range(4):
            pixels(t, slot).start()

    def moments(t, first):
        for slot in (first, first + 1):
            pixels(t, slot).wait()

        def block(index, carry):
            slot = first + index // 2
            half = index % 2
            start = pl.multiple_of(half * 32, 32)
            totals = [None] * MOMENTS
            for c in range(chans):
                x = pix[t, slot, c, pl.ds(start, 32), :]
                for k in range(MOMENTS):
                    term = coef[k * chans + c] * x
                    totals[k] = term if c == 0 else totals[k] + term
            for k in range(MOMENTS):
                part[t, slot, half, k] = totals[k]
            return carry

        lax.fori_loop(0, 4, block, 0)

    def make(t):
        moments(t, 0)
        core_copy(t).start()
        moments(t, 2)

    def join(t):
        core_copy(t).wait_recv()
        for side in range(2):
            for half in range(2):
                for k in range(MOMENTS):
                    part[t, 2 + side, half, k] = part[t, 2 + side, half, k] + got[t, side, half, k]
        far_copy(t).start()
        direct_copy(t).start()

    def row_sum(k, pieces):
        high, low = halves(jnp.concatenate(pieces, axis=0))
        band = row_band[k]
        return jnp.dot(band, high, preferred_element_type=F32) + jnp.dot(band, low, preferred_element_type=F32)

    def relay(t):
        direct_copy(t).wait_recv()
        to_other[t] = part[t, 3, half_other] + from_direct[t]
        other_copy(t).start()

    def give_rows(t):
        far_copy(t).wait_recv()
        blank = jnp.zeros((32, LANES), F32)
        for k in range(MOMENTS):
            to_direct[t, k] = row_sum(k, [part[t, 3, 0, k], part[t, 3, 1, k], from_same_far[t, k], blank])
        row_copy(t).start()

    def take_rows(t):
        own_copy(t).wait_recv()
        other_copy(t).wait_recv()
        sums = [
            row_sum(k, [part[t, 2, 0, k], part[t, 2, 1, k], from_same_own[t, k], from_other[t, k]])
            for k in range(MOMENTS)
        ]
        row_copy(t).wait_recv()
        for k in range(MOMENTS):
            rows[t + 1, k] = sums[k] + from_rows[t, k]

    def finish(t, scales):
        for k in range(MOMENTS):
            wide = jnp.concatenate([rows[t, k], rows[t + 1, k], rows[t + 2, k]], axis=1)
            high, low = halves(wide)
            band = col_band[k]
            total = jnp.dot(high, band, preferred_element_type=F32) + jnp.dot(low, band, preferred_element_type=F32)
            done[t, k] = (total.reshape(8, 8, LANES) * scales[k][None]).reshape(64, LANES)
        result(t).start()

    each(0, tiles, fetch)
    barrier = pltpu.get_barrier_semaphore()
    friends = (to_core, to_partner, to_far_core, to_wrap, to_wrap_other)
    for friend in friends:
        pl.semaphore_signal(barrier, inc=1, device_id=friend, device_id_type=MESH)

    weight_sum = F32(0)
    for c in range(chans):
        weight = weights[c].astype(F32)
        weight_sum = weight_sum + weight
        offset = offsets[c]
        value = weight
        for k in range(MOMENTS):
            coef[k * chans + c] = value
            value = value * offset
    w_mine[...] = jnp.full((8, LANES), weight_sum, F32)

    at_edge = jnp.logical_or(slab == 0, slab == slabs - 1)
    near = lax.broadcasted_iota(jnp.int32, (64, LANES), 0)
    lane = lax.broadcasted_iota(jnp.int32, (64, LANES), 1)
    same_shift = jnp.where(odd == 1, -96, 0)
    other_shift = jnp.where(at_edge, 1000, jnp.where(odd == 1, -32, -128))
    place = lane + jnp.where(lane < 64, 0, jnp.where(lane < 96, same_shift, other_shift))
    row_gap = jnp.abs(place - near)
    col_gap = jnp.abs(
        lax.broadcasted_iota(jnp.int32, (3 * LANES, LANES), 0) - LANES
        - lax.broadcasted_iota(jnp.int32, (3 * LANES, LANES), 1)
    )
    for k in range(MOMENTS):
        row_band[k] = jnp.where(row_gap <= reach[k], 1.0, 0.0).astype(BF16)
        col_band[k] = jnp.where(col_gap <= reach[k], 1.0, 0.0).astype(BF16)

    @pl.when(chan == 0)
    def _():
        rows[0] = jnp.zeros((MOMENTS, 64, LANES), F32)

    @pl.when(chan == 3)
    def _():
        rows[tiles + 1] = jnp.zeros((MOMENTS, 64, LANES), F32)

    pl.semaphore_wait(barrier, len(friends))
    make(tile_of(0))

    def making(order, carry):
        make(tile_of(order))
        join(tile_of(order - 1))
        return carry

    early = 2
    lax.fori_loop(1, early + 1, making, 0)
    each(0, early, lambda t: own_copy(t).start())
    for i in range(3):
        weight_copy(i).start()
    lax.fori_loop(early + 1, tiles, making, 0)
    join(tile_of(tiles - 1))

    def passing(t):
        relay(t)
        own_copy(t).start()
        give_rows(t)

    def passing_first(t):
        relay(t)
        give_rows(t)

    middle = max(early, (5 * tiles) // 8)
    each(0, early, passing_first)
    each(early, middle, passing)
    each(0, early, take_rows)

    @pl.when(chan > 0)
    def _():
        left_edge().start()

    @pl.when(chan < 3)
    def _():
        right_edge().start()

    each(middle, tiles, passing)

    for i in range(3):
        weight_copy(i).wait()
    total = w_mine[...] + w_got[0] + w_got[1] + w_got[2]
    scales = [1.0 / (total * (2 * reach[k] + 1).astype(F32)) for k in range(MOMENTS)]

    @pl.when(chan < 3)
    def _():
        left_edge().wait_recv()

    def finishing(order, carry):
        t = tile_of(order)
        take_rows(t)
        finish(t + 1, scales)
        return carry

    lax.fori_loop(early, tiles, finishing, 0)

    @pl.when(chan > 0)
    def _():
        right_edge().wait_recv()

    finish(1, scales)
    finish(0, scales)

    def drain(t):
        for copy in (core_copy, far_copy, own_copy, direct_copy, other_copy, row_copy):
            copy(t).wait_send()
        result(t).wait()

    each(0, tiles, drain)

    @pl.when(chan > 0)
    def _():
        left_edge().wait_send()

    @pl.when(chan < 3)
    def _():
        right_edge().wait_send()


def solution(mesh):
    slabs = mesh.shape["slab"]

    def body(beam, weights, offsets, reach):
        chans, height, width = beam.shape
        tiles = width // (4 * LANES)
        halo = (tiles, MOMENTS, 32, LANES)
        full = (MOMENTS, 64, LANES)
        dma = pltpu.SemaphoreType.DMA
        smem = pl.BlockSpec(memory_space=pltpu.SMEM)
        return pl.pallas_call(
            functools.partial(kernel, slabs, tiles, chans),
            out_shape=jax.ShapeDtypeStruct((MOMENTS, height, width // 4), F32),
            in_specs=[pl.BlockSpec(memory_space=pl.ANY), smem, smem, smem],
            out_specs=pl.BlockSpec(memory_space=pl.ANY),
            scratch_shapes=[
                pltpu.VMEM((tiles, 4, chans, 64, LANES), F32),
                pltpu.VMEM((tiles, 4, 2, MOMENTS, 32, LANES), F32),
                pltpu.VMEM((tiles, 2, 2, MOMENTS, 32, LANES), F32),
                pltpu.VMEM(halo, F32),
                pltpu.VMEM(halo, F32),
                pltpu.VMEM(halo, F32),
                pltpu.VMEM(halo, F32),
                pltpu.VMEM(halo, F32),
                pltpu.VMEM((tiles, *full), F32),
                pltpu.VMEM((tiles, *full), F32),
                pltpu.VMEM((tiles + 2, *full), F32),
                pltpu.VMEM((tiles, *full), F32),
                pltpu.VMEM((MOMENTS, 64, LANES), BF16),
                pltpu.VMEM((MOMENTS, 3 * LANES, LANES), BF16),
                pltpu.SMEM((MOMENTS * chans,), F32),
                pltpu.VMEM((8, LANES), F32),
                pltpu.VMEM((3, 8, LANES), F32),
                dma((tiles, 4)),
                dma((tiles,)), dma((tiles,)),
                dma((tiles,)), dma((tiles,)),
                dma((tiles,)), dma((tiles,)),
                dma((tiles,)), dma((tiles,)),
                dma((tiles,)), dma((tiles,)),
                dma((tiles,)), dma((tiles,)),
                dma((2,)), dma((2,)),
                dma((3,)), dma((3,)),
                dma((tiles,)),
            ],
            compiler_params=pltpu.CompilerParams(
                collective_id=0, has_side_effects=True, vmem_limit_bytes=60 * 1024 * 1024
            ),
        )(beam, weights, offsets, reach)

    placed = (P("chan", "slab", None), P("chan"), P("chan"), P())
    return jax.shard_map(
        body, mesh=mesh, in_specs=placed, out_specs=P(None, "slab", "chan"), check_vma=False
    )
```

time: 193 us -> 62.7 us (0.32)
  the two profiles are of different devices: /device:TPU:1 before, /device:TPU:3 now
where the time goes in v1:
time: 62.7 us; the launch traced here: 62.5 us
  Pallas kernels  60 us (96%)
  local copies, waits for them, and re-layouts  2.52 us (4%)
    pallas_call x1, Pallas kernels, body(): pl.pallas_call(functools.partial(kernel, slabs, tiles, chans), out_shape=...  60 us
    unnamed x1, local copies, waits for them, and re-layouts  2.52 us

profile of v1, /device:TPU:3, one launch (start us, length us, event | category | flops | bytes accessed | tf_op | source)
XLA Modules:
  0.0 62.5 jit_solution(672207083238774280)
XLA Ops:
  0.0 60.0 %shard_map.46 = f32[5,64,1024]{2,1,0:T(8,128)} custom-call(f32[16,64,4096]{2,1,0:T(8,128)} %beam.1, s32[16]{0:T(128)} %weights.1, f32[16]{0:T(128)} %offsets.1, s32[5]{0:T(128)} %reach.1), custom_call_target="tpu_custom_call" | custom-call | tf_op jit(solution)/shard_map/pallas_call | solution.py:305
  60.0 2.5 %copy.6 = f32[5,64,1024]{2,1,0:T(8,128)} copy(f32[5,64,1024]{2,1,0:T(8,128)} %shard_map.46) | data formatting | bytes 2621440

commit v2 on v1

--- a/solution.py
+++ b/solution.py
@@ -25,10 +25,10 @@
     slabs, tiles, chans,
     beam, weights, offsets, reach, out,
     pix, part, got, from_same_far, from_same_own, from_direct, to_other, from_other,
-    to_direct, from_rows, rows, done, row_band, col_band, coef, w_mine, w_got,
+    to_direct, from_rows, rows, row_band, col_band, coef, w_mine, w_pair, w_got,
     pix_sem, core_send, core_recv, far_send, far_recv, own_send, own_recv,
     dir_send, dir_recv, oth_send, oth_recv, row_send, row_recv,
-    edge_send, edge_recv, w_send, w_recv, out_sem,
+    edge_send, edge_recv, w_send, w_recv, ready, other_ready,
 ):
     chan = lax.axis_index("chan")
     slab = lax.axis_index("slab")
@@ -43,6 +43,10 @@
     to_core = (other_core, slab)
     to_partner = (partner, slab)
     to_far_core = (far_core, slab)
+    caller = jnp.logical_or(chan == 0, chan == 3)
+    callee = jnp.logical_not(caller)
+    at_edge = jnp.logical_or(slab == 0, slab == slabs - 1)
+    inside = jnp.logical_not(at_edge)
     to_wrap = (partner, same_slab)
     to_wrap_other = (partner, other_slab)
 
@@ -84,11 +88,7 @@
         return remote(rows.at[tiles], rows.at[0], edge_send.at[1], edge_recv.at[0], ((chan + 1) % 4, slab))
 
     def weight_copy(i):
-        return remote(w_mine, w_got.at[i], w_send.at[i], w_recv.at[i], (to_core, to_partner, to_far_core)[i])
-
-    def result(t):
-        start = pl.multiple_of(t * LANES, LANES)
-        return pltpu.make_async_copy(done.at[t], out.at[:, :, pl.ds(start, LANES)], out_sem.at[t])
+        return remote((w_mine, w_pair)[i], w_got.at[i], w_send.at[i], w_recv.at[i], (to_core, to_partner)[i])
 
     def each(first, last, body):
         def step(order, carry):
@@ -121,6 +121,10 @@
 
         lax.fori_loop(0, 4, block, 0)
 
+    def make_early(t):
+        moments(t, 0)
+        moments(t, 2)
+
     def make(t):
         moments(t, 0)
         core_copy(t).start()
@@ -143,7 +147,10 @@
     def relay(t):
         direct_copy(t).wait_recv()
         to_other[t] = part[t, 3, half_other] + from_direct[t]
-        other_copy(t).start()
+
+        @pl.when(inside)
+        def _():
+            other_copy(t).start()
 
     def give_rows(t):
         far_copy(t).wait_recv()
@@ -154,7 +161,11 @@
 
     def take_rows(t):
         own_copy(t).wait_recv()
-        other_copy(t).wait_recv()
+
+        @pl.when(inside)
+        def _():
+            other_copy(t).wait_recv()
+
         sums = [
             row_sum(k, [part[t, 2, 0, k], part[t, 2, 1, k], from_same_own[t, k], from_other[t, k]])
             for k in range(MOMENTS)
@@ -169,14 +180,27 @@
             high, low = halves(wide)
             band = col_band[k]
             total = jnp.dot(high, band, preferred_element_type=F32) + jnp.dot(low, band, preferred_element_type=F32)
-            done[t, k] = (total.reshape(8, 8, LANES) * scales[k][None]).reshape(64, LANES)
-        result(t).start()
+            start = pl.multiple_of(t * LANES, LANES)
+            out[k, :, pl.ds(start, LANES)] = (total.reshape(8, 8, LANES) * scales[k][None]).reshape(64, LANES)
 
     each(0, tiles, fetch)
     barrier = pltpu.get_barrier_semaphore()
-    friends = (to_core, to_partner, to_far_core, to_wrap, to_wrap_other)
-    for friend in friends:
-        pl.semaphore_signal(barrier, inc=1, device_id=friend, device_id_type=MESH)
+
+    def call(semaphore, where):
+        pl.semaphore_signal(semaphore, inc=1, device_id=where, device_id_type=MESH)
+
+    @pl.when(caller)
+    def _():
+        for friend in (to_core, to_partner, to_wrap):
+            call(barrier, friend)
+
+    @pl.when(callee)
+    def _():
+        call(barrier, to_far_core)
+
+    @pl.when(jnp.logical_and(callee, inside))
+    def _():
+        call(barrier, to_wrap_other)
 
     weight_sum = F32(0)
     for c in range(chans):
@@ -189,7 +213,28 @@
             value = value * offset
     w_mine[...] = jnp.full((8, LANES), weight_sum, F32)
 
-    at_edge = jnp.logical_or(slab == 0, slab == slabs - 1)
+    @pl.when(chan == 0)
+    def _():
+        rows[0] = jnp.zeros((MOMENTS, 64, LANES), F32)
+
+    @pl.when(chan == 3)
+    def _():
+        rows[tiles + 1] = jnp.zeros((MOMENTS, 64, LANES), F32)
+
+    @pl.when(at_edge)
+    def _():
+        from_other[...] = jnp.zeros_like(from_other)
+
+    early = 2
+    each(0, early, make_early)
+
+    @pl.when(callee)
+    def _():
+        pl.semaphore_wait(barrier, 4)
+        for friend in (to_core, to_partner, to_wrap):
+            call(ready, friend)
+        each(0, early, lambda t: core_copy(t).start())
+
     near = lax.broadcasted_iota(jnp.int32, (64, LANES), 0)
     lane = lax.broadcasted_iota(jnp.int32, (64, LANES), 1)
     same_shift = jnp.where(odd == 1, -96, 0)
@@ -204,42 +249,45 @@
         row_band[k] = jnp.where(row_gap <= reach[k], 1.0, 0.0).astype(BF16)
         col_band[k] = jnp.where(col_gap <= reach[k], 1.0, 0.0).astype(BF16)
 
-    @pl.when(chan == 0)
-    def _():
-        rows[0] = jnp.zeros((MOMENTS, 64, LANES), F32)
-
-    @pl.when(chan == 3)
-    def _():
-        rows[tiles + 1] = jnp.zeros((MOMENTS, 64, LANES), F32)
-
-    pl.semaphore_wait(barrier, len(friends))
-    make(tile_of(0))
+
+    @pl.when(caller)
+    def _():
+        pl.semaphore_wait(ready, 3)
+        each(0, early, lambda t: core_copy(t).start())
 
     def making(order, carry):
         make(tile_of(order))
-        join(tile_of(order - 1))
+        join(tile_of(order - early))
         return carry
 
-    early = 2
-    lax.fori_loop(1, early + 1, making, 0)
-    each(0, early, lambda t: own_copy(t).start())
-    for i in range(3):
-        weight_copy(i).start()
-    lax.fori_loop(early + 1, tiles, making, 0)
-    join(tile_of(tiles - 1))
+    weight_copy(0).start()
+    lax.fori_loop(early, tiles, making, 0)
+    each(tiles - early, tiles, join)
+    weight_copy(0).wait_recv()
+    w_pair[...] = w_mine[...] + w_got[0]
+
+    @pl.when(jnp.logical_and(caller, inside))
+    def _():
+        pl.semaphore_wait(barrier, 1)
+        call(other_ready, to_wrap_other)
+
+    @pl.when(jnp.logical_and(callee, inside))
+    def _():
+        pl.semaphore_wait(other_ready, 1)
 
     def passing(t):
         relay(t)
         own_copy(t).start()
         give_rows(t)
 
-    def passing_first(t):
+    def relaying(t):
         relay(t)
-        give_rows(t)
+        own_copy(t).start()
 
     middle = max(early, (5 * tiles) // 8)
-    each(0, early, passing_first)
-    each(early, middle, passing)
+    each(0, middle, passing)
+    each(middle, tiles, relaying)
+    weight_copy(1).start()
     each(0, early, take_rows)
 
     @pl.when(chan > 0)
@@ -250,11 +298,10 @@
     def _():
         right_edge().start()
 
-    each(middle, tiles, passing)
-
-    for i in range(3):
-        weight_copy(i).wait()
-    total = w_mine[...] + w_got[0] + w_got[1] + w_got[2]
+    each(middle, tiles, give_rows)
+
+    weight_copy(1).wait_recv()
+    total = w_pair[...] + w_got[1]
     scales = [1.0 / (total * (2 * reach[k] + 1).astype(F32)) for k in range(MOMENTS)]
 
     @pl.when(chan < 3)
@@ -277,11 +324,16 @@
     finish(0, scales)
 
     def drain(t):
-        for copy in (core_copy, far_copy, own_copy, direct_copy, other_copy, row_copy):
+        for copy in (core_copy, far_copy, own_copy, direct_copy, row_copy):
             copy(t).wait_send()
-        result(t).wait()
+
+        @pl.when(inside)
+        def _():
+            other_copy(t).wait_send()
 
     each(0, tiles, drain)
+    for i in range(2):
+        weight_copy(i).wait_send()
 
     @pl.when(chan > 0)
     def _():
@@ -304,9 +356,9 @@
         smem = pl.BlockSpec(memory_space=pltpu.SMEM)
         return pl.pallas_call(
             functools.partial(kernel, slabs, tiles, chans),
-            out_shape=jax.ShapeDtypeStruct((MOMENTS, height, width // 4), F32),
+            out_shape=pltpu.VMEM((MOMENTS, height, width // 4), F32),
             in_specs=[pl.BlockSpec(memory_space=pl.ANY), smem, smem, smem],
-            out_specs=pl.BlockSpec(memory_space=pl.ANY),
+            out_specs=pl.BlockSpec(memory_space=pltpu.VMEM),
             scratch_shapes=[
                 pltpu.VMEM((tiles, 4, chans, 64, LANES), F32),
                 pltpu.VMEM((tiles, 4, 2, MOMENTS, 32, LANES), F32),
@@ -319,12 +371,12 @@
                 pltpu.VMEM((tiles, *full), F32),
                 pltpu.VMEM((tiles, *full), F32),
                 pltpu.VMEM((tiles + 2, *full), F32),
-                pltpu.VMEM((tiles, *full), F32),
                 pltpu.VMEM((MOMENTS, 64, LANES), BF16),
                 pltpu.VMEM((MOMENTS, 3 * LANES, LANES), BF16),
                 pltpu.SMEM((MOMENTS * chans,), F32),
                 pltpu.VMEM((8, LANES), F32),
-                pltpu.VMEM((3, 8, LANES), F32),
+                pltpu.VMEM((8, LANES), F32),
+                pltpu.VMEM((2, 8, LANES), F32),
                 dma((tiles, 4)),
                 dma((tiles,)), dma((tiles,)),
                 dma((tiles,)), dma((tiles,)),
@@ -333,8 +385,8 @@
                 dma((tiles,)), dma((tiles,)),
                 dma((tiles,)), dma((tiles,)),
                 dma((2,)), dma((2,)),
-                dma((3,)), dma((3,)),
-                dma((tiles,)),
+                dma((2,)), dma((2,)),
+                pltpu.SemaphoreType.REGULAR, pltpu.SemaphoreType.REGULAR,
             ],
             compiler_params=pltpu.CompilerParams(
                 collective_id=0, has_side_effects=True, vmem_limit_bytes=60 * 1024 * 1024

time: 62.7 us -> 57.2 us (0.912)
  the two profiles are of different devices: /device:TPU:3 before, /device:TPU:24 now
where the time goes in v2:
time: 57.2 us; the launch traced here: 57.1 us
  Pallas kernels  56.1 us (98%)
  local copies, waits for them, and re-layouts  1.06 us (2%)
    pallas_call x1, Pallas kernels, body(): pl.pallas_call(functools.partial(kernel, slabs, tiles, chans), out_shape=...  56.1 us

profile of v2, /device:TPU:24, one launch (start us, length us, event | category | flops | bytes accessed | tf_op | source)
XLA Modules:
  0.0 57.1 jit_solution(17127159954792401404)
XLA Ops:
  0.0 56.1 %shard_map.46 = f32[5,64,1024]{2,1,0:T(8,128)S(1)} custom-call(f32[16,64,4096]{2,1,0:T(8,128)} %beam.1, s32[16]{0:T(128)} %weights.1, f32[16]{0:T(128)} %offsets.1, s32[5]{0:T(128)} %reach.1), custom_call_target="tpu_custom_call" | custom-call | tf_op jit(solution)/shard_map/pallas_call | solution.py:357
  56.1 1.1 %copy.6 = f32[5,64,1024]{2,1,0:T(8,128)} copy(f32[5,64,1024]{2,1,0:T(8,128)S(1)} %shard_map.46) | data formatting | bytes 2621440

commit v3 on v2

--- a/solution.py
+++ b/solution.py
@@ -25,7 +25,7 @@
     slabs, tiles, chans,
     beam, weights, offsets, reach, out,
     pix, part, got, from_same_far, from_same_own, from_direct, to_other, from_other,
-    to_direct, from_rows, rows, row_band, col_band, coef, w_mine, w_pair, w_got,
+    to_direct, from_rows, rows, row_band, col_band, coef, w_mine, w_pair, w_got, edge_mine, edge_got,
     pix_sem, core_send, core_recv, far_send, far_recv, own_send, own_recv,
     dir_send, dir_recv, oth_send, oth_recv, row_send, row_recv,
     edge_send, edge_recv, w_send, w_recv, ready, other_ready,
@@ -56,7 +56,11 @@
     def pixels(t, slot):
         quarter = (other_core, far_core, chan, partner)[slot]
         start = pl.multiple_of((quarter * tiles + t) * LANES, LANES)
-        return pltpu.make_async_copy(beam.at[:, :, pl.ds(start, LANES)], pix.at[t, slot], pix_sem.at[t, slot])
+        return pltpu.make_async_copy(beam.at[:, :, pl.ds(start, LANES)], pix.at[t, slot], pix_sem.at[t, slot // 2])
+
+    def pixels_wait(t, pair):
+        two = pix.at[t, pl.ds(2 * pair, 2)]
+        pltpu.make_async_copy(two, two, pix_sem.at[t, pair]).wait()
 
     def remote(src, dst, send, recv, where):
         return pltpu.make_async_remote_copy(
@@ -64,28 +68,28 @@
         )
 
     def core_copy(t):
-        return remote(part.at[t, pl.ds(0, 2)], got.at[t], core_send.at[t], core_recv.at[t], to_core)
+        return remote(part.at[t, pl.ds(0, 2)], got.at[t], core_send, core_recv.at[t], to_core)
 
     def far_copy(t):
-        return remote(part.at[t, 2, half_same], from_same_far.at[t], far_send.at[t], far_recv.at[t], to_wrap)
+        return remote(part.at[t, 2, half_same], from_same_far.at[t], far_send, far_recv.at[t], to_wrap)
 
     def own_copy(t):
-        return remote(part.at[t, 3, half_same], from_same_own.at[t], own_send.at[t], own_recv.at[t], to_wrap)
+        return remote(part.at[t, 3, half_same], from_same_own.at[t], own_send, own_recv.at[t], to_wrap)
 
     def direct_copy(t):
-        return remote(part.at[t, 2, half_other], from_direct.at[t], dir_send.at[t], dir_recv.at[t], to_partner)
+        return remote(part.at[t, 2, half_other], from_direct.at[t], dir_send, dir_recv.at[t], to_partner)
 
     def other_copy(t):
-        return remote(to_other.at[t], from_other.at[t], oth_send.at[t], oth_recv.at[t], to_wrap_other)
+        return remote(to_other.at[t], from_other.at[t], oth_send, oth_recv.at[t], to_wrap_other)
 
     def row_copy(t):
-        return remote(to_direct.at[t], from_rows.at[t], row_send.at[t], row_recv.at[t], to_partner)
+        return remote(to_direct.at[t], from_rows.at[t], row_send, row_recv.at[t], to_partner)
 
     def left_edge():
-        return remote(rows.at[1], rows.at[tiles + 1], edge_send.at[0], edge_recv.at[1], ((chan + 3) % 4, slab))
+        return remote(edge_mine.at[0], edge_got.at[1], edge_send.at[0], edge_recv.at[1], ((chan + 3) % 4, slab))
 
     def right_edge():
-        return remote(rows.at[tiles], rows.at[0], edge_send.at[1], edge_recv.at[0], ((chan + 1) % 4, slab))
+        return remote(edge_mine.at[1], edge_got.at[0], edge_send.at[1], edge_recv.at[0], ((chan + 1) % 4, slab))
 
     def weight_copy(i):
         return remote((w_mine, w_pair)[i], w_got.at[i], w_send.at[i], w_recv.at[i], (to_core, to_partner)[i])
@@ -102,8 +106,7 @@
             pixels(t, slot).start()
 
     def moments(t, first):
-        for slot in (first, first + 1):
-            pixels(t, slot).wait()
+        pixels_wait(t, first // 2)
 
         def block(index, carry):
             slot = first + index // 2
@@ -139,6 +142,26 @@
         far_copy(t).start()
         direct_copy(t).start()
 
+    lane_of = lax.broadcasted_iota(jnp.int32, (16, LANES), 1)
+
+    def pack(index, side, first):
+        for k in range(MOMENTS):
+            packed = jnp.zeros((16, LANES), F32)
+            for group in range(4):
+                piece = rows[index, k, pl.ds(16 * group, 16), :]
+                shift = (32 * group - first) % LANES
+                piece = piece if shift == 0 else pltpu.roll(piece, shift, 1)
+                packed = jnp.where(lane_of // 32 == group, piece, packed)
+            edge_mine[side, k] = packed
+
+    def unpack(index, side, first):
+        for k in range(MOMENTS):
+            packed = edge_got[side, k]
+            for group in range(4):
+                shift = (first - 32 * group) % LANES
+                piece = packed if shift == 0 else pltpu.roll(packed, shift, 1)
+                rows[index, k, pl.ds(16 * group, 16), :] = jnp.where(lane_of // 32 == first // 32, piece, 0.0)
+
     def row_sum(k, pieces):
         high, low = halves(jnp.concatenate(pieces, axis=0))
         band = row_band[k]
@@ -183,7 +206,6 @@
             start = pl.multiple_of(t * LANES, LANES)
             out[k, :, pl.ds(start, LANES)] = (total.reshape(8, 8, LANES) * scales[k][None]).reshape(64, LANES)
 
-    each(0, tiles, fetch)
     barrier = pltpu.get_barrier_semaphore()
 
     def call(semaphore, where):
@@ -201,6 +223,8 @@
     @pl.when(jnp.logical_and(callee, inside))
     def _():
         call(barrier, to_wrap_other)
+
+    each(0, tiles, fetch)
 
     weight_sum = F32(0)
     for c in range(chans):
@@ -213,58 +237,66 @@
             value = value * offset
     w_mine[...] = jnp.full((8, LANES), weight_sum, F32)
 
-    @pl.when(chan == 0)
-    def _():
-        rows[0] = jnp.zeros((MOMENTS, 64, LANES), F32)
-
-    @pl.when(chan == 3)
-    def _():
-        rows[tiles + 1] = jnp.zeros((MOMENTS, 64, LANES), F32)
-
-    @pl.when(at_edge)
-    def _():
-        from_other[...] = jnp.zeros_like(from_other)
-
-    early = 2
-    each(0, early, make_early)
-
-    @pl.when(callee)
-    def _():
-        pl.semaphore_wait(barrier, 4)
-        for friend in (to_core, to_partner, to_wrap):
-            call(ready, friend)
-        each(0, early, lambda t: core_copy(t).start())
-
     near = lax.broadcasted_iota(jnp.int32, (64, LANES), 0)
     lane = lax.broadcasted_iota(jnp.int32, (64, LANES), 1)
     same_shift = jnp.where(odd == 1, -96, 0)
     other_shift = jnp.where(at_edge, 1000, jnp.where(odd == 1, -32, -128))
     place = lane + jnp.where(lane < 64, 0, jnp.where(lane < 96, same_shift, other_shift))
     row_gap = jnp.abs(place - near)
+    for k in range(MOMENTS):
+        row_band[k] = jnp.where(row_gap <= reach[k], 1.0, 0.0).astype(BF16)
+
+    @pl.when(callee)
+    def _():
+        pl.semaphore_wait(barrier, 4)
+        for friend in (to_core, to_partner, to_wrap):
+            call(ready, friend)
+
+    moments(tile_of(0), 0)
+
+    @pl.when(caller)
+    def _():
+        pl.semaphore_wait(ready, 3)
+
+    weight_copy(0).start()
+    core_copy(tile_of(0)).start()
+    moments(tile_of(0), 2)
+
+    def making(order, carry):
+        t = tile_of(order)
+        moments(t, 0)
+        core_copy(t).start()
+        join(tile_of(order - 1))
+        moments(t, 2)
+        return carry
+
+    lax.fori_loop(1, 2, making, 0)
+    weight_copy(0).wait_recv()
+    w_pair[...] = w_mine[...] + w_got[0]
+    lax.fori_loop(2, 3, making, 0)
+    weight_copy(1).start()
+    lax.fori_loop(3, tiles, making, 0)
+
     col_gap = jnp.abs(
         lax.broadcasted_iota(jnp.int32, (3 * LANES, LANES), 0) - LANES
         - lax.broadcasted_iota(jnp.int32, (3 * LANES, LANES), 1)
     )
     for k in range(MOMENTS):
-        row_band[k] = jnp.where(row_gap <= reach[k], 1.0, 0.0).astype(BF16)
         col_band[k] = jnp.where(col_gap <= reach[k], 1.0, 0.0).astype(BF16)
 
-
-    @pl.when(caller)
-    def _():
-        pl.semaphore_wait(ready, 3)
-        each(0, early, lambda t: core_copy(t).start())
-
-    def making(order, carry):
-        make(tile_of(order))
-        join(tile_of(order - early))
-        return carry
-
-    weight_copy(0).start()
-    lax.fori_loop(early, tiles, making, 0)
-    each(tiles - early, tiles, join)
-    weight_copy(0).wait_recv()
-    w_pair[...] = w_mine[...] + w_got[0]
+    @pl.when(at_edge)
+    def _():
+        from_other[...] = jnp.zeros_like(from_other)
+
+    @pl.when(chan == 0)
+    def _():
+        rows[0] = jnp.zeros((MOMENTS, 64, LANES), F32)
+
+    @pl.when(chan == 3)
+    def _():
+        rows[tiles + 1] = jnp.zeros((MOMENTS, 64, LANES), F32)
+
+    join(tile_of(tiles - 1))
 
     @pl.when(jnp.logical_and(caller, inside))
     def _():
@@ -284,18 +316,20 @@
         relay(t)
         own_copy(t).start()
 
+    early = 2
     middle = max(early, (5 * tiles) // 8)
     each(0, middle, passing)
     each(middle, tiles, relaying)
-    weight_copy(1).start()
     each(0, early, take_rows)
 
     @pl.when(chan > 0)
     def _():
+        pack(1, 0, 0)
         left_edge().start()
 
     @pl.when(chan < 3)
     def _():
+        pack(tiles, 1, 96)
         right_edge().start()
 
     each(middle, tiles, give_rows)
@@ -307,6 +341,7 @@
     @pl.when(chan < 3)
     def _():
         left_edge().wait_recv()
+        unpack(tiles + 1, 1, 0)
 
     def finishing(order, carry):
         t = tile_of(order)
@@ -319,19 +354,24 @@
     @pl.when(chan > 0)
     def _():
         right_edge().wait_recv()
+        unpack(0, 0, 96)
 
     finish(1, scales)
     finish(0, scales)
 
-    def drain(t):
-        for copy in (core_copy, far_copy, own_copy, direct_copy, row_copy):
-            copy(t).wait_send()
-
-        @pl.when(inside)
-        def _():
-            other_copy(t).wait_send()
-
-    each(0, tiles, drain)
+    def sent(buffer, send):
+        pltpu.make_async_copy(buffer, buffer, send).wait()
+
+    sent(got, core_send)
+    sent(from_same_far, far_send)
+    sent(from_same_own, own_send)
+    sent(from_direct, dir_send)
+    sent(from_rows, row_send)
+
+    @pl.when(inside)
+    def _():
+        sent(from_other, oth_send)
+
     for i in range(2):
         weight_copy(i).wait_send()
 
@@ -377,13 +417,15 @@
                 pltpu.VMEM((8, LANES), F32),
                 pltpu.VMEM((8, LANES), F32),
                 pltpu.VMEM((2, 8, LANES), F32),
-                dma((tiles, 4)),
-                dma((tiles,)), dma((tiles,)),
-                dma((tiles,)), dma((tiles,)),
-                dma((tiles,)), dma((tiles,)),
-                dma((tiles,)), dma((tiles,)),
-                dma((tiles,)), dma((tiles,)),
-                dma((tiles,)), dma((tiles,)),
+                pltpu.VMEM((2, MOMENTS, 16, LANES), F32),
+                pltpu.VMEM((2, MOMENTS, 16, LANES), F32),
+                dma((tiles, 2)),
+                dma, dma((tiles,)),
+                dma, dma((tiles,)),
+                dma, dma((tiles,)),
+                dma, dma((tiles,)),
+                dma, dma((tiles,)),
+                dma, dma((tiles,)),
                 dma((2,)), dma((2,)),
                 dma((2,)), dma((2,)),
                 pltpu.SemaphoreType.REGULAR, pltpu.SemaphoreType.REGULAR,

time: 57.2 us -> 55.5 us (0.970)
  Pallas kernels: 56.1 us -> 54.3 us
    pallas_call x1, Pallas kernels: 56.1 us -> 54.3 us  [body(): pl.pallas_call(functools.partial(kernel, slabs, tiles, chans), out_shape=...]
where the time goes in v3:
time: 55.5 us; the launch traced here: 55.4 us
  Pallas kernels  54.3 us (98%)
  local copies, waits for them, and re-layouts  1.06 us (2%)
    pallas_call x1, Pallas kernels, body(): pl.pallas_call(functools.partial(kernel, slabs, tiles, chans), out_shape=...  54.3 us

profile of v3, /device:TPU:24, one launch (start us, length us, event | category | flops | bytes accessed | tf_op | source)
XLA Modules:
  0.0 55.4 jit_solution(177411066052124439)
XLA Ops:
  0.0 54.3 %shard_map.46 = f32[5,64,1024]{2,1,0:T(8,128)S(1)} custom-call(f32[16,64,4096]{2,1,0:T(8,128)} %beam.1, s32[16]{0:T(128)} %weights.1, f32[16]{0:T(128)} %offsets.1, s32[5]{0:T(128)} %reach.1), custom_call_target="tpu_custom_call" | custom-call | tf_op jit(solution)/shard_map/pallas_call | solution.py:397
  54.3 1.1 %copy.6 = f32[5,64,1024]{2,1,0:T(8,128)} copy(f32[5,64,1024]{2,1,0:T(8,128)S(1)} %shard_map.46) | data formatting | bytes 2621440

commit v4 on v3

--- a/solution.py
+++ b/solution.py
@@ -24,10 +24,10 @@
 def kernel(
     slabs, tiles, chans,
     beam, weights, offsets, reach, out,
-    pix, part, got, from_same_far, from_same_own, from_direct, to_other, from_other,
-    to_direct, from_rows, rows, row_band, col_band, coef, w_mine, w_pair, w_got, edge_mine, edge_got,
-    pix_sem, core_send, core_recv, far_send, far_recv, own_send, own_recv,
-    dir_send, dir_recv, oth_send, oth_recv, row_send, row_recv,
+    pix, part, got, raw_got, same_got, other_got, edge_same, edge_other, to_direct, from_rows,
+    rows, row_band, col_band, coef, w_mine, w_pair, w_got, edge_mine, edge_got,
+    pix_sem, core_send, core_recv, raw_send, raw_recv, same_send, same_recv, other_send, other_recv,
+    es_send, es_recv, eo_send, eo_recv, row_send, row_recv,
     edge_send, edge_recv, w_send, w_recv, ready, other_ready,
 ):
     chan = lax.axis_index("chan")
@@ -43,15 +43,23 @@
     to_core = (other_core, slab)
     to_partner = (partner, slab)
     to_far_core = (far_core, slab)
+    to_wrap = (partner, same_slab)
+    to_wrap_other = (partner, other_slab)
     caller = jnp.logical_or(chan == 0, chan == 3)
     callee = jnp.logical_not(caller)
     at_edge = jnp.logical_or(slab == 0, slab == slabs - 1)
     inside = jnp.logical_not(at_edge)
-    to_wrap = (partner, same_slab)
-    to_wrap_other = (partner, other_slab)
-
-    def tile_of(order):
-        return (tiles - order) % tiles
+
+    inner = (tiles - 2) // 2
+    OWN, OTH = 2, 3
+
+    def away(i):
+        return (1 + i) * (1 - odd) + (tiles - 2 - i) * odd
+
+    def home(i):
+        return (1 + i) * odd + (tiles - 2 - i) * (1 - odd)
+
+    edge_tile = (0, tiles - 1)
 
     def pixels(t, slot):
         quarter = (other_core, far_core, chan, partner)[slot]
@@ -70,20 +78,29 @@
     def core_copy(t):
         return remote(part.at[t, pl.ds(0, 2)], got.at[t], core_send, core_recv.at[t], to_core)
 
-    def far_copy(t):
-        return remote(part.at[t, 2, half_same], from_same_far.at[t], far_send, far_recv.at[t], to_wrap)
-
-    def own_copy(t):
-        return remote(part.at[t, 3, half_same], from_same_own.at[t], own_send, own_recv.at[t], to_wrap)
-
-    def direct_copy(t):
-        return remote(part.at[t, 2, half_other], from_direct.at[t], dir_send, dir_recv.at[t], to_partner)
-
-    def other_copy(t):
-        return remote(to_other.at[t], from_other.at[t], oth_send, oth_recv.at[t], to_wrap_other)
+    def raw_copy(t, slot):
+        return remote(part.at[t, slot], raw_got.at[t], raw_send, raw_recv.at[t], to_partner)
+
+    def same_copy(t, slot):
+        return remote(part.at[t, slot, half_same], same_got.at[t], same_send, same_recv.at[t], to_wrap)
+
+    def other_copy(t, slot):
+        return remote(part.at[t, slot, half_other], other_got.at[t], other_send, other_recv.at[t], to_wrap_other)
+
+    def edge_same_copy(e, slot):
+        src = part.at[edge_tile[e], slot, half_same]
+        return remote(src, edge_same.at[e, slot - 2], es_send, es_recv.at[e, slot - 2], to_wrap)
+
+    def edge_other_copy(e, slot):
+        src = part.at[edge_tile[e], slot, half_other]
+        return remote(src, edge_other.at[e, slot - 2], eo_send, eo_recv.at[e, slot - 2], to_wrap_other)
+
+    def edge_row_copy(e):
+        t = edge_tile[e]
+        return remote(to_direct.at[t], from_rows.at[e], row_send, row_recv.at[t], to_partner)
 
     def row_copy(t):
-        return remote(to_direct.at[t], from_rows.at[t], row_send, row_recv.at[t], to_partner)
+        return remote(to_direct.at[t], rows.at[t + 1], row_send, row_recv.at[t], to_partner)
 
     def left_edge():
         return remote(edge_mine.at[0], edge_got.at[1], edge_send.at[0], edge_recv.at[1], ((chan + 3) % 4, slab))
@@ -93,13 +110,6 @@
 
     def weight_copy(i):
         return remote((w_mine, w_pair)[i], w_got.at[i], w_send.at[i], w_recv.at[i], (to_core, to_partner)[i])
-
-    def each(first, last, body):
-        def step(order, carry):
-            body(tile_of(order))
-            return carry
-
-        lax.fori_loop(first, last, step, 0)
 
     def fetch(t):
         for slot in range(4):
@@ -124,23 +134,29 @@
 
         lax.fori_loop(0, 4, block, 0)
 
-    def make_early(t):
-        moments(t, 0)
-        moments(t, 2)
-
-    def make(t):
-        moments(t, 0)
-        core_copy(t).start()
-        moments(t, 2)
-
     def join(t):
         core_copy(t).wait_recv()
-        for side in range(2):
-            for half in range(2):
-                for k in range(MOMENTS):
-                    part[t, 2 + side, half, k] = part[t, 2 + side, half, k] + got[t, side, half, k]
-        far_copy(t).start()
-        direct_copy(t).start()
+
+        def add(index, carry):
+            side = index // 2
+            half = index % 2
+            for k in range(MOMENTS):
+                part[t, 2 + side, half, k] = part[t, 2 + side, half, k] + got[t, side, half, k]
+            return carry
+
+        lax.fori_loop(0, 4, add, 0)
+
+    def complete(t, slot):
+        raw_copy(t, slot).wait_recv()
+        for half in range(2):
+            for k in range(MOMENTS):
+                part[t, slot, half, k] = part[t, slot, half, k] + raw_got[t, half, k]
+
+        @pl.when(inside)
+        def _():
+            other_copy(t, slot).start()
+
+        same_copy(t, slot).start()
 
     lane_of = lax.broadcasted_iota(jnp.int32, (16, LANES), 1)
 
@@ -167,43 +183,54 @@
         band = row_band[k]
         return jnp.dot(band, high, preferred_element_type=F32) + jnp.dot(band, low, preferred_element_type=F32)
 
-    def relay(t):
-        direct_copy(t).wait_recv()
-        to_other[t] = part[t, 3, half_other] + from_direct[t]
+    def tile_rows(t, slot, dst, at):
+        same_copy(t, slot).wait_recv()
 
         @pl.when(inside)
         def _():
-            other_copy(t).start()
-
-    def give_rows(t):
-        far_copy(t).wait_recv()
-        blank = jnp.zeros((32, LANES), F32)
-        for k in range(MOMENTS):
-            to_direct[t, k] = row_sum(k, [part[t, 3, 0, k], part[t, 3, 1, k], from_same_far[t, k], blank])
+            other_copy(t, slot).wait_recv()
+
+        for k in range(MOMENTS):
+            dst[at, k] = row_sum(k, [part[t, slot, 0, k], part[t, slot, 1, k], same_got[t, k], other_got[t, k]])
+
+    def give_back(t):
+        tile_rows(t, OTH, to_direct, t)
         row_copy(t).start()
 
-    def take_rows(t):
-        own_copy(t).wait_recv()
+    def edge_sums(e, slot):
+        t = edge_tile[e]
+        theirs = OWN + OTH - slot
+        edge_same_copy(e, theirs).wait_recv()
 
         @pl.when(inside)
         def _():
-            other_copy(t).wait_recv()
-
-        sums = [
-            row_sum(k, [part[t, 2, 0, k], part[t, 2, 1, k], from_same_own[t, k], from_other[t, k]])
+            edge_other_copy(e, theirs).wait_recv()
+
+        i = theirs - 2
+        return [
+            row_sum(k, [part[t, slot, 0, k], part[t, slot, 1, k], edge_same[e, i, k], edge_other[e, i, k]])
             for k in range(MOMENTS)
         ]
-        row_copy(t).wait_recv()
-        for k in range(MOMENTS):
-            rows[t + 1, k] = sums[k] + from_rows[t, k]
+
+    def edge_give(e):
+        sums = edge_sums(e, OTH)
+        for k in range(MOMENTS):
+            to_direct[edge_tile[e], k] = sums[k]
+        edge_row_copy(e).start()
+
+    def edge_take(e):
+        sums = edge_sums(e, OWN)
+        edge_row_copy(e).wait_recv()
+        for k in range(MOMENTS):
+            rows[edge_tile[e] + 1, k] = sums[k] + from_rows[e, k]
 
     def finish(t, scales):
+        start = pl.multiple_of(t * LANES, LANES)
         for k in range(MOMENTS):
             wide = jnp.concatenate([rows[t, k], rows[t + 1, k], rows[t + 2, k]], axis=1)
             high, low = halves(wide)
             band = col_band[k]
             total = jnp.dot(high, band, preferred_element_type=F32) + jnp.dot(low, band, preferred_element_type=F32)
-            start = pl.multiple_of(t * LANES, LANES)
             out[k, :, pl.ds(start, LANES)] = (total.reshape(8, 8, LANES) * scales[k][None]).reshape(64, LANES)
 
     barrier = pltpu.get_barrier_semaphore()
@@ -224,7 +251,17 @@
     def _():
         call(barrier, to_wrap_other)
 
-    each(0, tiles, fetch)
+    order = []
+    for i in range(max(inner, 2)):
+        if i < inner:
+            order.append(("away", away(i)))
+        if i < 2:
+            order.append(("edge", edge_tile[i]))
+        if i < inner:
+            order.append(("home", home(i)))
+    ahead = 3
+    for _, t in order[:ahead]:
+        fetch(t)
 
     weight_sum = F32(0)
     for c in range(chans):
@@ -252,41 +289,49 @@
         for friend in (to_core, to_partner, to_wrap):
             call(ready, friend)
 
-    moments(tile_of(0), 0)
-
-    @pl.when(caller)
-    def _():
-        pl.semaphore_wait(ready, 3)
-
-    weight_copy(0).start()
-    core_copy(tile_of(0)).start()
-    moments(tile_of(0), 2)
-
-    def making(order, carry):
-        t = tile_of(order)
+    def joined(kind, t):
+        join(t)
+        if kind == "away":
+            raw_copy(t, OWN).start()
+        elif kind == "home":
+            raw_copy(t, OTH).start()
+        elif kind == "edge":
+            edge_same_copy(edge_tile.index(t), OWN).start()
+            edge_same_copy(edge_tile.index(t), OTH).start()
+
+    for i, (kind, t) in enumerate(order):
         moments(t, 0)
+        if i == 0:
+
+            @pl.when(caller)
+            def _():
+                pl.semaphore_wait(ready, 3)
+
+            weight_copy(0).start()
         core_copy(t).start()
-        join(tile_of(order - 1))
+        if i + ahead < len(order):
+            fetch(order[i + ahead][1])
+        if i > 0:
+            joined(*order[i - 1])
         moments(t, 2)
-        return carry
-
-    lax.fori_loop(1, 2, making, 0)
-    weight_copy(0).wait_recv()
-    w_pair[...] = w_mine[...] + w_got[0]
-    lax.fori_loop(2, 3, making, 0)
-    weight_copy(1).start()
-    lax.fori_loop(3, tiles, making, 0)
-
-    col_gap = jnp.abs(
-        lax.broadcasted_iota(jnp.int32, (3 * LANES, LANES), 0) - LANES
-        - lax.broadcasted_iota(jnp.int32, (3 * LANES, LANES), 1)
-    )
-    for k in range(MOMENTS):
-        col_band[k] = jnp.where(col_gap <= reach[k], 1.0, 0.0).astype(BF16)
+        if i == 1:
+            weight_copy(0).wait_recv()
+            w_pair[...] = w_mine[...] + w_got[0]
+        if i == 2:
+            weight_copy(1).start()
+        if i == 2 + inner:
+            col_gap = jnp.abs(
+                lax.broadcasted_iota(jnp.int32, (3 * LANES, LANES), 0) - LANES
+                - lax.broadcasted_iota(jnp.int32, (3 * LANES, LANES), 1)
+            )
+            for k in range(MOMENTS):
+                col_band[k] = jnp.where(col_gap <= reach[k], 1.0, 0.0).astype(BF16)
+    joined(*order[-1])
 
     @pl.when(at_edge)
     def _():
-        from_other[...] = jnp.zeros_like(from_other)
+        other_got[...] = jnp.zeros_like(other_got)
+        edge_other[...] = jnp.zeros_like(edge_other)
 
     @pl.when(chan == 0)
     def _():
@@ -295,8 +340,6 @@
     @pl.when(chan == 3)
     def _():
         rows[tiles + 1] = jnp.zeros((MOMENTS, 64, LANES), F32)
-
-    join(tile_of(tiles - 1))
 
     @pl.when(jnp.logical_and(caller, inside))
     def _():
@@ -307,20 +350,34 @@
     def _():
         pl.semaphore_wait(other_ready, 1)
 
-    def passing(t):
-        relay(t)
-        own_copy(t).start()
-        give_rows(t)
-
-    def relaying(t):
-        relay(t)
-        own_copy(t).start()
-
-    early = 2
-    middle = max(early, (5 * tiles) // 8)
-    each(0, middle, passing)
-    each(middle, tiles, relaying)
-    each(0, early, take_rows)
+    def edge_others(slot):
+        @pl.when(inside)
+        def _():
+            for e in range(2):
+                edge_other_copy(e, slot).start()
+
+    def complete_pair(i):
+        complete(away(i), OTH)
+        complete(home(i), OWN)
+
+    def rows_pair(i):
+        give_back(away(i))
+        tile_rows(home(i), OWN, rows, home(i) + 1)
+
+    edge_others(OWN)
+    complete_pair(0)
+    edge_others(OTH)
+    for i in range(1, inner - 1):
+        complete_pair(i)
+    for e in range(2):
+        edge_give(e)
+    rows_pair(0)
+    if inner > 1:
+        complete_pair(inner - 1)
+    for i in range(1, inner - 1):
+        rows_pair(i)
+    for e in range(2):
+        edge_take(e)
 
     @pl.when(chan > 0)
     def _():
@@ -332,7 +389,8 @@
         pack(tiles, 1, 96)
         right_edge().start()
 
-    each(middle, tiles, give_rows)
+    if inner > 1:
+        rows_pair(inner - 1)
 
     weight_copy(1).wait_recv()
     total = w_pair[...] + w_got[1]
@@ -343,34 +401,37 @@
         left_edge().wait_recv()
         unpack(tiles + 1, 1, 0)
 
-    def finishing(order, carry):
-        t = tile_of(order)
-        take_rows(t)
-        finish(t + 1, scales)
-        return carry
-
-    lax.fori_loop(early, tiles, finishing, 0)
-
     @pl.when(chan > 0)
     def _():
         right_edge().wait_recv()
         unpack(0, 0, 96)
 
-    finish(1, scales)
-    finish(0, scales)
+    out_step = 1 - 2 * odd
+
+    def last_steps(i, carry):
+        finish(home(i) + out_step, scales)
+        row_copy(away(i)).wait_recv()
+        finish(away(i) - out_step, scales)
+        return carry
+
+    lax.fori_loop(0, inner, last_steps, 0)
+    finish(home(inner - 1), scales)
+    finish(away(inner - 1), scales)
 
     def sent(buffer, send):
         pltpu.make_async_copy(buffer, buffer, send).wait()
 
+    middle = pl.ds(1, tiles - 2)
     sent(got, core_send)
-    sent(from_same_far, far_send)
-    sent(from_same_own, own_send)
-    sent(from_direct, dir_send)
-    sent(from_rows, row_send)
+    sent(raw_got.at[middle], raw_send)
+    sent(same_got.at[middle], same_send)
+    sent(edge_same, es_send)
+    sent(rows.at[pl.ds(0, inner + 2)], row_send)
 
     @pl.when(inside)
     def _():
-        sent(from_other, oth_send)
+        sent(other_got.at[middle], other_send)
+        sent(edge_other, eo_send)
 
     for i in range(2):
         weight_copy(i).wait_send()
@@ -390,7 +451,7 @@
     def body(beam, weights, offsets, reach):
         chans, height, width = beam.shape
         tiles = width // (4 * LANES)
-        halo = (tiles, MOMENTS, 32, LANES)
+        halo = (MOMENTS, 32, LANES)
         full = (MOMENTS, 64, LANES)
         dma = pltpu.SemaphoreType.DMA
         smem = pl.BlockSpec(memory_space=pltpu.SMEM)
@@ -401,15 +462,15 @@
             out_specs=pl.BlockSpec(memory_space=pltpu.VMEM),
             scratch_shapes=[
                 pltpu.VMEM((tiles, 4, chans, 64, LANES), F32),
-                pltpu.VMEM((tiles, 4, 2, MOMENTS, 32, LANES), F32),
-                pltpu.VMEM((tiles, 2, 2, MOMENTS, 32, LANES), F32),
-                pltpu.VMEM(halo, F32),
-                pltpu.VMEM(halo, F32),
-                pltpu.VMEM(halo, F32),
-                pltpu.VMEM(halo, F32),
-                pltpu.VMEM(halo, F32),
+                pltpu.VMEM((tiles, 4, 2, *halo), F32),
+                pltpu.VMEM((tiles, 2, 2, *halo), F32),
+                pltpu.VMEM((tiles, 2, *halo), F32),
+                pltpu.VMEM((tiles, *halo), F32),
+                pltpu.VMEM((tiles, *halo), F32),
+                pltpu.VMEM((2, 2, *halo), F32),
+                pltpu.VMEM((2, 2, *halo), F32),
                 pltpu.VMEM((tiles, *full), F32),
-                pltpu.VMEM((tiles, *full), F32),
+                pltpu.VMEM((2, *full), F32),
                 pltpu.VMEM((tiles + 2, *full), F32),
                 pltpu.VMEM((MOMENTS, 64, LANES), BF16),
                 pltpu.VMEM((MOMENTS, 3 * LANES, LANES), BF16),
@@ -424,7 +485,8 @@
                 dma, dma((tiles,)),
                 dma, dma((tiles,)),
                 dma, dma((tiles,)),
-                dma, dma((tiles,)),
+                dma, dma((2, 2)),
+                dma, dma((2, 2)),
                 dma, dma((tiles,)),
                 dma((2,)), dma((2,)),
                 dma((2,)), dma((2,)),

time: 55.5 us -> 54 us (0.973)
  Pallas kernels: 54.3 us -> 52.3 us
    pallas_call x1, Pallas kernels: 54.3 us -> 52.3 us  [body(): pl.pallas_call(functools.partial(kernel, slabs, tiles, chans), out_shape=...]
where the time goes in v4:
time: 54 us; the launch traced here: 53.4 us
  Pallas kernels  52.3 us (97%)
  local copies, waits for them, and re-layouts  1.06 us (2%)
    pallas_call x1, Pallas kernels, body(): pl.pallas_call(functools.partial(kernel, slabs, tiles, chans), out_shape=...  52.3 us

profile of v4, /device:TPU:24, one launch (start us, length us, event | category | flops | bytes accessed | tf_op | source)
XLA Modules:
  0.0 53.4 jit_solution(13866407131014093962)
XLA Ops:
  0.0 52.3 %shard_map.46 = f32[5,64,1024]{2,1,0:T(8,128)S(1)} custom-call(f32[16,64,4096]{2,1,0:T(8,128)} %beam.1, s32[16]{0:T(128)} %weights.1, f32[16]{0:T(128)} %offsets.1, s32[5]{0:T(128)} %reach.1), custom_call_target="tpu_custom_call" | custom-call | tf_op jit(solution)/shard_map/pallas_call | solution.py:458
  52.3 1.1 %copy.6 = f32[5,64,1024]{2,1,0:T(8,128)} copy(f32[5,64,1024]{2,1,0:T(8,128)S(1)} %shard_map.46) | data formatting | bytes 2621440

commit v5 on v4

--- a/solution.py
+++ b/solution.py
@@ -254,13 +254,13 @@
     order = []
     for i in range(max(inner, 2)):
         if i < inner:
-            order.append(("away", away(i)))
+            order.append(("away", i, away(i)))
         if i < 2:
-            order.append(("edge", edge_tile[i]))
+            order.append(("edge", i, edge_tile[i]))
         if i < inner:
-            order.append(("home", home(i)))
+            order.append(("home", i, home(i)))
     ahead = 3
-    for _, t in order[:ahead]:
+    for _, _, t in order[:ahead]:
         fetch(t)
 
     weight_sum = F32(0)
@@ -289,17 +289,18 @@
         for friend in (to_core, to_partner, to_wrap):
             call(ready, friend)
 
-    def joined(kind, t):
+    last = inner - 1
+
+    def joined(kind, i, t):
         join(t)
-        if kind == "away":
-            raw_copy(t, OWN).start()
-        elif kind == "home":
-            raw_copy(t, OTH).start()
-        elif kind == "edge":
-            edge_same_copy(edge_tile.index(t), OWN).start()
-            edge_same_copy(edge_tile.index(t), OTH).start()
-
-    for i, (kind, t) in enumerate(order):
+        if kind == "edge":
+            edge_same_copy(i, OWN).start()
+            if i == 0:
+                edge_same_copy(i, OTH).start()
+        elif i < last or last == 0:
+            raw_copy(t, OWN if kind == "away" else OTH).start()
+
+    for i, (kind, at, t) in enumerate(order):
         moments(t, 0)
         if i == 0:
 
@@ -310,7 +311,7 @@
             weight_copy(0).start()
         core_copy(t).start()
         if i + ahead < len(order):
-            fetch(order[i + ahead][1])
+            fetch(order[i + ahead][2])
         if i > 0:
             joined(*order[i - 1])
         moments(t, 2)
@@ -365,17 +366,28 @@
         tile_rows(home(i), OWN, rows, home(i) + 1)
 
     edge_others(OWN)
-    complete_pair(0)
-    edge_others(OTH)
-    for i in range(1, inner - 1):
-        complete_pair(i)
+    for i in range(last):
+        complete(away(i), OTH)
+        complete(home(i), OWN)
+        if i == 0:
+            raw_copy(home(last), OTH).start()
+            raw_copy(away(last), OWN).start()
     for e in range(2):
         edge_give(e)
-    rows_pair(0)
-    if inner > 1:
-        complete_pair(inner - 1)
-    for i in range(1, inner - 1):
+
+    def rows_pair(i):
+        give_back(away(i))
+        tile_rows(home(i), OWN, rows, home(i) + 1)
+
+    if last > 0:
+        rows_pair(0)
+    complete(home(last), OWN)
+    edge_same_copy(1, OTH).start()
+    edge_others(OTH)
+    complete(away(last), OTH)
+    for i in range(1, last):
         rows_pair(i)
+    give_back(away(last))
     for e in range(2):
         edge_take(e)
 
@@ -389,9 +401,7 @@
         pack(tiles, 1, 96)
         right_edge().start()
 
-    if inner > 1:
-        rows_pair(inner - 1)
-
+    tile_rows(home(last), OWN, rows, home(last) + 1)
     weight_copy(1).wait_recv()
     total = w_pair[...] + w_got[1]
     scales = [1.0 / (total * (2 * reach[k] + 1).astype(F32)) for k in range(MOMENTS)]

time: 54 us -> 54 us (level)
  no operation moved by 1% of the time
where the time goes in v5:
time: 54 us; the launch traced here: 53.5 us
  Pallas kernels  52.4 us (97%)
  local copies, waits for them, and re-layouts  1.06 us (2%)
    pallas_call x1, Pallas kernels, body(): pl.pallas_call(functools.partial(kernel, slabs, tiles, chans), out_shape=...  52.4 us

profile of v5, /device:TPU:24, one launch (start us, length us, event | category | flops | bytes accessed | tf_op | source)
XLA Modules:
  0.0 53.5 jit_solution(15736560458066645114)
XLA Ops:
  0.0 52.4 %shard_map.46 = f32[5,64,1024]{2,1,0:T(8,128)S(1)} custom-call(f32[16,64,4096]{2,1,0:T(8,128)} %beam.1, s32[16]{0:T(128)} %weights.1, f32[16]{0:T(128)} %offsets.1, s32[5]{0:T(128)} %reach.1), custom_call_target="tpu_custom_call" | custom-call | tf_op jit(solution)/shard_map/pallas_call | solution.py:468
  52.4 1.1 %copy.6 = f32[5,64,1024]{2,1,0:T(8,128)} copy(f32[5,64,1024]{2,1,0:T(8,128)S(1)} %shard_map.46) | data formatting | bytes 2621440

commit v6 on v5

--- a/solution.py
+++ b/solution.py
@@ -290,6 +290,7 @@
             call(ready, friend)
 
     last = inner - 1
+    long = inner >= 3
 
     def joined(kind, i, t):
         join(t)
@@ -297,8 +298,31 @@
             edge_same_copy(i, OWN).start()
             if i == 0:
                 edge_same_copy(i, OTH).start()
-        elif i < last or last == 0:
+        elif i == 0 or (i < last and not (long and i == 1 and kind == "away")):
             raw_copy(t, OWN if kind == "away" else OTH).start()
+
+    def edge_others(slot):
+        @pl.when(inside)
+        def _():
+            for e in range(2):
+                edge_other_copy(e, slot).start()
+
+    def meet():
+        @pl.when(jnp.logical_and(caller, inside))
+        def _():
+            pl.semaphore_wait(barrier, 1)
+            call(other_ready, to_wrap_other)
+
+    def first_pair():
+        @pl.when(jnp.logical_and(callee, inside))
+        def _():
+            pl.semaphore_wait(other_ready, 1)
+
+        edge_others(OWN)
+        complete(away(0), OTH)
+        if long:
+            raw_copy(away(1), OWN).start()
+        edge_others(OTH)
 
     for i, (kind, at, t) in enumerate(order):
         moments(t, 0)
@@ -320,6 +344,9 @@
             w_pair[...] = w_mine[...] + w_got[0]
         if i == 2:
             weight_copy(1).start()
+            meet()
+        if i == 5 and long:
+            first_pair()
         if i == 2 + inner:
             col_gap = jnp.abs(
                 lax.broadcasted_iota(jnp.int32, (3 * LANES, LANES), 0) - LANES
@@ -342,49 +369,28 @@
     def _():
         rows[tiles + 1] = jnp.zeros((MOMENTS, 64, LANES), F32)
 
-    @pl.when(jnp.logical_and(caller, inside))
-    def _():
-        pl.semaphore_wait(barrier, 1)
-        call(other_ready, to_wrap_other)
-
-    @pl.when(jnp.logical_and(callee, inside))
-    def _():
-        pl.semaphore_wait(other_ready, 1)
-
-    def edge_others(slot):
-        @pl.when(inside)
-        def _():
-            for e in range(2):
-                edge_other_copy(e, slot).start()
-
-    def complete_pair(i):
+    if not long:
+        first_pair()
+    complete(home(0), OWN)
+    if last > 0:
+        raw_copy(home(last), OTH).start()
+        raw_copy(away(last), OWN).start()
+    for i in range(1, last):
         complete(away(i), OTH)
         complete(home(i), OWN)
+    for e in range(2):
+        edge_give(e)
 
     def rows_pair(i):
         give_back(away(i))
         tile_rows(home(i), OWN, rows, home(i) + 1)
 
-    edge_others(OWN)
-    for i in range(last):
-        complete(away(i), OTH)
-        complete(home(i), OWN)
-        if i == 0:
-            raw_copy(home(last), OTH).start()
-            raw_copy(away(last), OWN).start()
-    for e in range(2):
-        edge_give(e)
-
-    def rows_pair(i):
-        give_back(away(i))
-        tile_rows(home(i), OWN, rows, home(i) + 1)
-
     if last > 0:
         rows_pair(0)
-    complete(home(last), OWN)
+        complete(home(last), OWN)
     edge_same_copy(1, OTH).start()
-    edge_others(OTH)
-    complete(away(last), OTH)
+    if last > 0:
+        complete(away(last), OTH)
     for i in range(1, last):
         rows_pair(i)
     give_back(away(last))

time: 54 us -> 51.5 us (0.954)
  Pallas kernels: 52.4 us -> 50.3 us
    pallas_call x1, Pallas kernels: 52.4 us -> 50.3 us  [body(): pl.pallas_call(functools.partial(kernel, slabs, tiles, chans), out_shape=...]
where the time goes in v6:
time: 51.5 us; the launch traced here: 51.4 us
  Pallas kernels  50.3 us (98%)
  local copies, waits for them, and re-layouts  1.06 us (2%)
    pallas_call x1, Pallas kernels, body(): pl.pallas_call(functools.partial(kernel, slabs, tiles, chans), out_shape=...  50.3 us
    unnamed x1, local copies, waits for them, and re-layouts  1.06 us

profile of v6, /device:TPU:24, one launch (start us, length us, event | category | flops | bytes accessed | tf_op | source)
XLA Modules:
  0.0 51.4 jit_solution(11479647437614416119)
XLA Ops:
  0.0 50.3 %shard_map.46 = f32[5,64,1024]{2,1,0:T(8,128)S(1)} custom-call(f32[16,64,4096]{2,1,0:T(8,128)} %beam.1, s32[16]{0:T(128)} %weights.1, f32[16]{0:T(128)} %offsets.1, s32[5]{0:T(128)} %reach.1), custom_call_target="tpu_custom_call" | custom-call | tf_op jit(solution)/shard_map/pallas_call | solution.py:474
  50.3 1.1 %copy.6 = f32[5,64,1024]{2,1,0:T(8,128)} copy(f32[5,64,1024]{2,1,0:T(8,128)S(1)} %shard_map.46) | data formatting | bytes 2621440

commit v7 on v6

--- a/solution.py
+++ b/solution.py
@@ -296,8 +296,7 @@
         join(t)
         if kind == "edge":
             edge_same_copy(i, OWN).start()
-            if i == 0:
-                edge_same_copy(i, OTH).start()
+            edge_same_copy(i, OTH).start()
         elif i == 0 or (i < last and not (long and i == 1 and kind == "away")):
             raw_copy(t, OWN if kind == "away" else OTH).start()
 
@@ -388,12 +387,12 @@
     if last > 0:
         rows_pair(0)
         complete(home(last), OWN)
-    edge_same_copy(1, OTH).start()
     if last > 0:
         complete(away(last), OTH)
     for i in range(1, last):
         rows_pair(i)
-    give_back(away(last))
+    if last == 0:
+        give_back(away(last))
     for e in range(2):
         edge_take(e)
 
@@ -407,32 +406,47 @@
         pack(tiles, 1, 96)
         right_edge().start()
 
-    tile_rows(home(last), OWN, rows, home(last) + 1)
+    if last > 0:
+        give_back(away(last))
+
     weight_copy(1).wait_recv()
     total = w_pair[...] + w_got[1]
     scales = [1.0 / (total * (2 * reach[k] + 1).astype(F32)) for k in range(MOMENTS)]
-
-    @pl.when(chan < 3)
-    def _():
-        left_edge().wait_recv()
-        unpack(tiles + 1, 1, 0)
-
-    @pl.when(chan > 0)
-    def _():
-        right_edge().wait_recv()
-        unpack(0, 0, 96)
-
     out_step = 1 - 2 * odd
 
-    def last_steps(i, carry):
+    def home_step(i, carry):
         finish(home(i) + out_step, scales)
+        return carry
+
+    def away_step(i, carry):
         row_copy(away(i)).wait_recv()
         finish(away(i) - out_step, scales)
         return carry
 
-    lax.fori_loop(0, inner, last_steps, 0)
-    finish(home(inner - 1), scales)
-    finish(away(inner - 1), scales)
+    lax.fori_loop(1, last, home_step, 0)
+    if last > 0:
+        row_copy(away(0)).wait_recv()
+    lax.fori_loop(1, last, away_step, 0)
+    tile_rows(home(last), OWN, rows, home(last) + 1)
+    lax.fori_loop(max(last, 1), last + 1, home_step, 0)
+    if last > 0:
+        lax.fori_loop(last, last + 1, away_step, 0)
+    else:
+        row_copy(away(0)).wait_recv()
+    finish(home(last), scales)
+    finish(away(last), scales)
+
+    @pl.when(chan > 0)
+    def _():
+        right_edge().wait_recv()
+        unpack(0, 0, 96)
+
+    @pl.when(chan < 3)
+    def _():
+        left_edge().wait_recv()
+        unpack(tiles + 1, 1, 0)
+
+    lax.fori_loop(0, 2, lambda e, carry: (finish(e * (tiles - 1), scales), carry)[1], 0)
 
     def sent(buffer, send):
         pltpu.make_async_copy(buffer, buffer, send).wait()

time: 51.5 us -> 51.3 us (level)
  no operation moved by 1% of the time
where the time goes in v7:
time: 51.3 us; the launch traced here: 51.2 us
  Pallas kernels  50.1 us (98%)
  local copies, waits for them, and re-layouts  1.06 us (2%)
    pallas_call x1, Pallas kernels, body(): pl.pallas_call(functools.partial(kernel, slabs, tiles, chans), out_shape=...  50.1 us
    unnamed x1, local copies, waits for them, and re-layouts  1.06 us

profile of v7, /device:TPU:24, one launch (start us, length us, event | category | flops | bytes accessed | tf_op | source)
XLA Modules:
  0.0 51.2 jit_solution(18236297672894212009)
XLA Ops:
  0.0 50.1 %shard_map.46 = f32[5,64,1024]{2,1,0:T(8,128)S(1)} custom-call(f32[16,64,4096]{2,1,0:T(8,128)} %beam.1, s32[16]{0:T(128)} %weights.1, f32[16]{0:T(128)} %offsets.1, s32[5]{0:T(128)} %reach.1), custom_call_target="tpu_custom_call" | custom-call | tf_op jit(solution)/shard_map/pallas_call | solution.py:488
  50.1 1.1 %copy.6 = f32[5,64,1024]{2,1,0:T(8,128)} copy(f32[5,64,1024]{2,1,0:T(8,128)S(1)} %shard_map.46) | data formatting | bytes 2621440
